TPU v7x, 128 devices: a whole 4x4x4 slice. The times are simulated.
128 devices in a mesh: tri: 2 (over x_hi), blk: 64 (over y, x_lo, z, core).
Axes of the slice: x: 4 (x_hi: 2, x_lo: 2; x = x_hi * 2 + x_lo), y: 4, z: 4, core: 2. Of those that a mesh axis runs over, the one named last changes fastest.
Arguments:
- layers: float32 [384, 4, 393216], P(('tri', 'blk')), as said below
- tile_mask: int32 [384, 1, 24], P(('tri', 'blk')), may hold values 0 or 1
- depth_order: int32 [384], replicated, may hold values from 0 to 383, as said below
Outputs:
- composite: float32 [4, 393216], P(None, 'blk')
Inputs may be any that keep to these rules, and one draw needn't show every extreme that they name: `layers`: in each rank's layer the first three channels lie between 0 and channel 3, and channel 3 lies between 0 and 6 / 384. `depth_order`: A permutation. Ranks are numbered so that device d of the mesh (tri index times 64 plus blk index) holds ranks 3 * d to 3 * d + 2, and these take consecutive positions. The 64 devices of one tri index hold consecutive positions, and for every bit b, the devices of one tri index that agree on all bits of the blk index above bit b hold consecutive positions.
All inputs are finite; a program needn't handle non-finite values. No bound on the sum of `tile_mask` on one device may be relied on, other than what follows from the above.
Results may differ from a plain program's by a relative error of at most 0.00002.
Values sent between devices are 32-bit elements; how exact they have to be, the bound alone decides.
A program may use at most 128 MiB of HBM per device.

v0:
```python
import jax
import jax.numpy as jnp
from jax import lax
from jax.sharding import PartitionSpec as P

WIDTH = 3072
TILE = 128


def blend_pair(nearer, farther):
    return nearer + (1.0 - nearer[3:4]) * farther


def blend_ordered(ordered):
    while ordered.shape[1] > 1:
        paired = ordered.reshape(4, ordered.shape[1] // 2, 2, ordered.shape[2])
        ordered = blend_pair(paired[:, :, 0], paired[:, :, 1])
    return ordered[:, 0]


def blend_group(stacked, depths):
    members = stacked.shape[1]
    summed = jnp.zeros_like(stacked[:, 0])
    for source in range(members):
        through = jnp.ones_like(stacked[3, 0])
        for other in range(members):
            if other != source:
                through = through * jnp.where(
                    depths[other] < depths[source], 1.0 - stacked[3, other], 1.0
                )
        summed = summed + through[None] * stacked[:, source]
    return summed


def on_device(layers, tile_mask, depth_order):
    blk_count = lax.axis_size("blk")
    tri_count = lax.axis_size("tri")
    blk_index = lax.axis_index("blk")
    tri_index = lax.axis_index("tri")
    device_index = tri_index * blk_count + blk_index
    rank_dev = layers.shape[0]
    pixels = layers.shape[2]
    tile_rows = pixels // WIDTH // TILE
    tile_on = tile_mask.astype(jnp.float32)
    masked = (
        layers.reshape(rank_dev, 4, tile_rows, TILE, WIDTH // TILE, TILE)
        * tile_on[:, None, :, None, :, None]
    )
    masked = masked.reshape(rank_dev, 4, pixels)
    own_depths = lax.dynamic_slice_in_dim(depth_order, device_index * rank_dev, rank_dev)
    local_image = blend_group(jnp.moveaxis(masked, 0, 1), own_depths)
    device_depth = jnp.min(depth_order.reshape(-1, rank_dev), axis=1)
    partial_value = local_image.reshape(4, blk_count, pixels // blk_count)
    received = lax.all_to_all(partial_value, "blk", split_axis=1, concat_axis=1, tiled=True)
    group_depths = lax.dynamic_slice_in_dim(device_depth, tri_index * blk_count, blk_count)
    position = (group_depths - jnp.min(group_depths)) // rank_dev
    inverse = (
        jnp.zeros((blk_count,), jnp.int32).at[position].set(jnp.arange(blk_count, dtype=jnp.int32))
    )
    ordered = jnp.take(received, inverse, axis=1)
    own_block = blend_ordered(ordered)
    group_devices = jnp.arange(tri_count, dtype=jnp.int32) * blk_count + blk_index
    tri_depths = device_depth[group_devices]
    gathered = lax.all_gather(own_block[:, None, :], "tri", axis=1, tiled=True)
    composite = blend_group(gathered, tri_depths)
    return composite


def solution(mesh):
    in_specs = (P(("tri", "blk"), None, None), P(("tri", "blk"), None, None), P())
    out_specs = P(None, "blk")
    return jax.shard_map(
        on_device, mesh=mesh, in_specs=in_specs, out_specs=out_specs, check_vma=False
    )
```

profile of v0, /device:TPU:32, one launch (start us, length us, event | category | flops | bytes accessed | tf_op | source)
XLA Modules:
  0.0 227.3 jit_solution(562508941444263034)
XLA Ops:
  0.0 0.8 dynamic_slice.7
  0.8 0.6 fusion.29
  8.9 0.7 convert_element_type.3
  9.6 0.4 mul.178
  10.0 14.3 %copy.26 = f32[1,3,3072,128]{3,1,2,0:T(4,128)} copy(f32[1,3,3072,128]{3,2,1,0:T(8,128)S(1)} %bitcast.97) | data formatting | bytes 9437184
  24.3 19.1 %multiply_bitcast_fusion = f32[4,3,393216]{2,0,1:T(4,128)} fusion(f32[3,4,393216]{2,1,0:T(4,128)} %param.3, f32[3,393216]{1,0:T(4,128)} %bitcast.96), kind=kLoop, calls=%fused_computation.3 | loop fusion | flops 4718592 | bytes 42467328 | tf_op jit(solution)/shard_map/transpose | solution.py:51
  43.4 13.8 %fusion.23 = (f32[4,1,393216]{2,0,1:T(4,128)}, f32[4,1,393216]{2,0,1:T(4,128)}, f32[4,1,393216]{2,0,1:T(4,128)}) fusion(f32[4,3,393216]{2,0,1:T(4,128)} %multiply_bitcast_fusion), kind=kLoop, calls=%fused_computation.69 | loop fusion | bytes 37748736 | tf_op jit(solution)/shard_map/slice | solution.py:31
  57.3 22.5 %fusion.1 = (f32[393216]{0:T(1024)S(1)}, f32[393216]{0:T(1024)}, f32[393216]{0:T(1024)}) fusion(pred[]{:T(512)} %bitcast.2, pred[]{:T(512)} %bitcast.4, f32[4,3,393216]{2,0,1:T(4,128)} %multiply_bitcast_fusion, pred[]{:T(512)} %bitcast.10, pred[]{:T(512)} %bitcast.9, pred[]{:T(512)} %bitcast.7, pred[]{:T(512)} %bitcast.6), kind=kLoop, calls=%fused_computation.15 | loop fusion | flops 4718592 | bytes 9437190 | tf_op jit(solution)/shard_map/mul | solution.py:28
  79.9 1.6 mul.187
  81.5 2.6 %mul.191 = f32[64,6144]{1,0:T(8,128)} reshape(f32[393216]{0:T(1024)} %get-tuple-element.6) | data formatting | bytes 3145728 | tf_op jit(solution)/shard_map/mul | solution.py:28
  84.1 12.7 %multiply_add_fusion = f32[4,64,6144]{2,0,1:T(4,128)} fusion(f32[4,64,6144]{2,0,1:T(4,128)} %bitcast.93, f32[4,64,6144]{2,0,1:T(4,128)} %bitcast.94, f32[4,64,6144]{2,0,1:T(4,128)} %bitcast.92, f32[64,6144]{1,0:T(8,128)} %mul.191, f32[64,6144]{1,0:T(8,128)S(1)} %mul.187, f32[64,6144]{1,0:T(8,128)S(1)} %mul.183), kind=kLoop, calls=%fused_computation.6 | loop fusion | flops 7864320 | bytes 29884416 | tf_op jit(solution)/shard_map/add | solution.py:31
  96.8 9.8 %all-to-all-start = ((f32[4,64,6144]{2,0,1:T(4,128)}), f32[4,64,6144]{2,0,1:T(4,128)}, u32[]{:S(2)}, u32[]{:S(2)}) async-start(f32[4,64,6144]{2,0,1:T(4,128)} %multiply_add_fusion), calls=%async_computation | async-start | bytes 12582912 | tf_op jit(solution)/shard_map/all_to_all | solution.py:54
  107.0 0.6 gather_fusion
  107.6 0.6 fusion.28
  110.8 0.7 dynamic-slice_reduce_fusion
  111.5 0.7 compare_select_fusion.1
  112.2 0.8 scatter_custom_fusion
  113.2 75.1 %all-to-all-done = f32[4,64,6144]{2,0,1:T(4,128)} async-done(((f32[4,64,6144]{2,0,1:T(4,128)}), f32[4,64,6144]{2,0,1:T(4,128)}, u32[]{:S(2)}, u32[]{:S(2)}) %all-to-all-start) | async-done | bytes 6291488 | tf_op jit(solution)/shard_map/all_to_all | solution.py:54
  188.4 9.4 %gather_fusion.1 = f32[64,4,6144]{2,1,0:T(4,128)} fusion(f32[4,64,6144]{2,0,1:T(4,128)} %all-to-all-done, s32[1024]{0:T(1024)S(1)} %pad_clamp_fusion), kind=kCustom, calls=%fused_computation.1 | custom fusion | bytes 12583168 | tf_op jit(solution)/shard_map/jit(_take)/gather | solution.py:60
  197.7 4.5 %copy_select_fusion = f32[4,32,2,6144]{3,0,1,2:T(4,128)S(1)} fusion(f32[4,32,2,6144]{3,0,2,1:T(4,128)} %bitcast.95, pred[32,2]{0,1:T(4,128)(4,1)S(1)} %copy.11), kind=kLoop, calls=%fused_computation.5 | loop fusion | flops 1572864 | bytes 12582976 | tf_op jit(solution)/shard_map/jit(_take)/select_n | solution.py:60
  202.2 2.1 fusion.24
  204.3 3.3 %fusion.7 = f32[32,6144]{1,0:T(8,128)} fusion(f32[4,32,2,6144]{3,0,1,2:T(4,128)S(1)} %copy_select_fusion), kind=kLoop, calls=%fused_computation.26 | loop fusion | flops 196608 | bytes 1572864 | tf_op jit(solution)/shard_map/sub | solution.py:11
  207.6 2.5 %sub.154 = f32[16,2,6144]{2,1,0:T(2,128)} reshape(f32[32,6144]{1,0:T(8,128)} %fusion.7) | data formatting | bytes 1572864 | tf_op jit(solution)/shard_map/sub | solution.py:11
  210.1 3.3 %multiply_add_fusion.1 = f32[4,16,2,6144]{3,0,2,1:T(4,128)S(1)} fusion(f32[4,16,2,6144]{3,0,2,1:T(4,128)} %bitcast.99, f32[4,16,2,6144]{3,0,2,1:T(4,128)S(1)} %bitcast.98, f32[16,2,6144]{2,1,0:T(2,128)} %sub.154), kind=kLoop, calls=%fused_computation.7 | loop fusion | flops 1572864 | bytes 10223616 | tf_op jit(solution)/shard_map/add | solution.py:11
  213.6 1.9 fusion.9
  215.6 1.2 sub.157
  216.8 0.9 fusion.6
  217.8 0.6 fusion.13
  218.5 0.3 fusion.8
  218.9 0.3 fusion.19
  219.7 6.8 %all_gather.3 = f32[4,2,6144]{2,0,1:T(4,128)S(1)} all-gather(f32[4,1,6144]{2,0,1:T(4,128)S(1)} %fusion.18), channel_id=1, replica_groups=mesh['tri'=2,'blk'=64] {'tri'}, dimensions={1}, use_global_device_ids=true | all-gather | bytes 294912 | tf_op jit(solution)/shard_map/all_gather | solution.py:64
  226.6 0.7 fusion.15
  (26 shorter events, 1.9 us)
Async XLA Ops:
  96.8 9.8 %copy-start = (s32[384]{0:T(512)S(1)}, s32[384]{0:T(512)}, u32[]{:S(2)}) copy-start(s32[384]{0:T(512)} %param.5) | copy-start | bytes 4612
  96.8 91.6 %all-to-all-start = ((f32[4,64,6144]{2,0,1:T(4,128)}), f32[4,64,6144]{2,0,1:T(4,128)}, u32[]{:S(2)}, u32[]{:S(2)}) async-start(f32[4,64,6144]{2,0,1:T(4,128)} %multiply_add_fusion), calls=%async_computation | async-start | bytes 12582912 | tf_op jit(solution)/shard_map/all_to_all | solution.py:54
where the time goes:
time: 228 us; the launch traced here: 227 us
  waiting for transfers between devices  75.1 us (33%)
  other arithmetic  72.7 us (32%)
  local copies, waits for them, and re-layouts  52.4 us (23%)
  between operations  10.4 us (5%)
  starting transfers between devices  9.83 us (4%)
  blocking collectives  6.79 us (3%)
    all_to_all x1, waiting for transfers between devices, on_device(): lax.all_to_all(partial_value, 'blk', split_axis=1, concat_axis=1, tiled=T...  75.1 us
    mul x1, other arithmetic, blend_group(): through * jnp.where(depths[other] < depths[source], 1.0 - stacked[3, othe...  22.5 us
    transpose x1, other arithmetic, on_device(): local_image = blend_group(jnp.moveaxis(masked, 0, 1), own_depths)  19.1 us
    unnamed x5, local copies, waits for them, and re-layouts  14.4 us
    slice x1, local copies, waits for them, and re-layouts, blend_group(): summed = summed + through[None] * stacked[:, source]  13.8 us
    add x2, other arithmetic, blend_group(): summed = summed + through[None] * stacked[:, source]  13.4 us
    all_to_all x1, starting transfers between devices, on_device(): lax.all_to_all(partial_value, 'blk', split_axis=1, concat_axis=1, tiled=T...  9.83 us
    gather x1, local copies, waits for them, and re-layouts, on_device(): ordered = jnp.take(received, inverse, axis=1)  9.36 us
  transfers between devices with their start and end apart: 1, of which 1 were waited for; matrix products, arithmetic and copies ran while one was open for 2% of the time, Pallas kernels for 0%

commit v1 on v0

--- a/solution.py
+++ b/solution.py
@@ -61,7 +61,10 @@
     own_block = blend_ordered(ordered)
     group_devices = jnp.arange(tri_count, dtype=jnp.int32) * blk_count + blk_index
     tri_depths = device_depth[group_devices]
-    gathered = lax.all_gather(own_block[:, None, :], "tri", axis=1, tiled=True)
+    gathered = jnp.concatenate(
+        lax.all_to_all(jnp.stack([own_block[:, None, :]] * lax.axis_size("tri")), "tri", 0, 0),
+        axis=1,
+    )
     composite = blend_group(gathered, tri_depths)
     return composite
 

time: 228 us -> 232 us (1.018)
  blocking collectives: 6.79 us -> 0 us
  waiting for transfers between devices: 75.1 us -> 81.6 us
  starting transfers between devices: 9.83 us -> 13.8 us
    all_gather x1 -> x0, blocking collectives: 6.79 us -> none  [on_device(): gathered = lax.all_gather(own_block[:, None, :], 'tri', axis=1, tiled=True)]
    all_to_all x0 -> x1, starting transfers between devices: none -> 4 us  [on_device(): lax.all_to_all(jnp.stack([own_block[:, None, :]] * lax.axis_size('tri')),...]
    all_to_all x0 -> x1, waiting for transfers between devices: none -> 3.33 us  [on_device(): lax.all_to_all(jnp.stack([own_block[:, None, :]] * lax.axis_size('tri')),...]
    all_to_all x1, waiting for transfers between devices: 75.1 us -> 78.3 us  [on_device(): lax.all_to_all(partial_value, 'blk', split_axis=1, concat_axis=1, tiled=T...]
  transfers between devices with their start and end apart: 1 -> 2, of which waited for: 1 -> 2; matrix products, arithmetic and copies ran while one was open for 2% -> 2% of each run, Pallas kernels for 0% -> 0%
where the time goes in v1:
time: 232 us
  waiting for transfers between devices  81.6 us (35%)
  other arithmetic  73.4 us (32%)
  local copies, waits for them, and re-layouts  52.4 us (23%)
  starting transfers between devices  13.8 us (6%)
  between operations  10.2 us (4%)
    all_to_all x1, waiting for transfers between devices, on_device(): lax.all_to_all(partial_value, 'blk', split_axis=1, concat_axis=1, tiled=T...  78.3 us
    mul x1, other arithmetic, blend_group(): through * jnp.where(depths[other] < depths[source], 1.0 - stacked[3, othe...  22.5 us
    transpose x1, other arithmetic, on_device(): local_image = blend_group(jnp.moveaxis(masked, 0, 1), own_depths)  19.1 us
    unnamed x5, local copies, waits for them, and re-layouts  14.4 us
    slice x1, local copies, waits for them, and re-layouts, blend_group(): summed = summed + through[None] * stacked[:, source]  13.8 us
    add x2, other arithmetic, blend_group(): summed = summed + through[None] * stacked[:, source]  13.4 us
    all_to_all x1, starting transfers between devices, on_device(): lax.all_to_all(partial_value, 'blk', split_axis=1, concat_axis=1, tiled=T...  9.83 us
    gather x1, local copies, waits for them, and re-layouts, on_device(): ordered = jnp.take(received, inverse, axis=1)  9.36 us
  transfers between devices with their start and end apart: 2, of which 2 were waited for; matrix products, arithmetic and copies ran while one was open for 2% of the time, Pallas kernels for 0%

profile of v1, /device:TPU:32, one launch (start us, length us, event | category | flops | bytes accessed | tf_op | source)
XLA Modules:
  0.0 231.5 jit_solution(3422038413661824106)
XLA Ops:
  0.0 0.8 dynamic_slice.7
  0.8 0.6 fusion.29
  8.9 0.7 convert_element_type.3
  9.6 0.4 mul.179
  10.0 14.3 %copy.24 = f32[1,3,3072,128]{3,1,2,0:T(4,128)} copy(f32[1,3,3072,128]{3,2,1,0:T(8,128)S(1)} %bitcast.100) | data formatting | bytes 9437184
  24.3 19.1 %multiply_bitcast_fusion = f32[4,3,393216]{2,0,1:T(4,128)} fusion(f32[3,4,393216]{2,1,0:T(4,128)} %param.3, f32[3,393216]{1,0:T(4,128)} %bitcast.99), kind=kLoop, calls=%fused_computation.3 | loop fusion | flops 4718592 | bytes 42467328 | tf_op jit(solution)/shard_map/transpose | solution.py:51
  43.4 13.8 %fusion.23 = (f32[4,1,393216]{2,0,1:T(4,128)}, f32[4,1,393216]{2,0,1:T(4,128)}, f32[4,1,393216]{2,0,1:T(4,128)}) fusion(f32[4,3,393216]{2,0,1:T(4,128)} %multiply_bitcast_fusion), kind=kLoop, calls=%fused_computation.70 | loop fusion | bytes 37748736 | tf_op jit(solution)/shard_map/slice | solution.py:31
  57.3 22.5 %fusion.1 = (f32[393216]{0:T(1024)S(1)}, f32[393216]{0:T(1024)}, f32[393216]{0:T(1024)}) fusion(pred[]{:T(512)} %bitcast.2, pred[]{:T(512)} %bitcast.4, f32[4,3,393216]{2,0,1:T(4,128)} %multiply_bitcast_fusion, pred[]{:T(512)} %bitcast.10, pred[]{:T(512)} %bitcast.9, pred[]{:T(512)} %bitcast.7, pred[]{:T(512)} %bitcast.6), kind=kLoop, calls=%fused_computation.15 | loop fusion | flops 4718592 | bytes 9437190 | tf_op jit(solution)/shard_map/mul | solution.py:28
  79.9 1.6 mul.188
  81.5 2.6 %mul.192 = f32[64,6144]{1,0:T(8,128)} reshape(f32[393216]{0:T(1024)} %get-tuple-element.6) | data formatting | bytes 3145728 | tf_op jit(solution)/shard_map/mul | solution.py:28
  84.1 12.7 %multiply_add_fusion = f32[4,64,6144]{2,0,1:T(4,128)} fusion(f32[4,64,6144]{2,0,1:T(4,128)} %bitcast.96, f32[4,64,6144]{2,0,1:T(4,128)} %bitcast.97, f32[4,64,6144]{2,0,1:T(4,128)} %bitcast.95, f32[64,6144]{1,0:T(8,128)} %mul.192, f32[64,6144]{1,0:T(8,128)S(1)} %mul.188, f32[64,6144]{1,0:T(8,128)S(1)} %mul.184), kind=kLoop, calls=%fused_computation.6 | loop fusion | flops 7864320 | bytes 29884416 | tf_op jit(solution)/shard_map/add | solution.py:31
  96.8 9.8 %all-to-all-start = ((f32[4,64,6144]{2,0,1:T(4,128)}), f32[4,64,6144]{2,0,1:T(4,128)}, u32[]{:S(2)}, u32[]{:S(2)}) async-start(f32[4,64,6144]{2,0,1:T(4,128)} %multiply_add_fusion), calls=%async_computation | async-start | bytes 12582912 | tf_op jit(solution)/shard_map/all_to_all | solution.py:54
  107.0 0.7 dynamic-slice_reduce_fusion
  107.7 0.7 compare_select_fusion.1
  108.4 0.8 scatter_custom_fusion
  109.5 0.6 gather_fusion
  110.1 78.3 %all-to-all-done = f32[4,64,6144]{2,0,1:T(4,128)} async-done(((f32[4,64,6144]{2,0,1:T(4,128)}), f32[4,64,6144]{2,0,1:T(4,128)}, u32[]{:S(2)}, u32[]{:S(2)}) %all-to-all-start) | async-done | bytes 6291488 | tf_op jit(solution)/shard_map/all_to_all | solution.py:54
  188.4 9.4 %gather_fusion.1 = f32[64,4,6144]{2,1,0:T(4,128)} fusion(f32[4,64,6144]{2,0,1:T(4,128)} %all-to-all-done, s32[1024]{0:T(1024)S(1)} %pad_clamp_fusion), kind=kCustom, calls=%fused_computation.1 | custom fusion | bytes 12583168 | tf_op jit(solution)/shard_map/jit(_take)/gather | solution.py:60
  197.7 4.5 %copy_select_fusion = f32[4,32,2,6144]{3,0,1,2:T(4,128)S(1)} fusion(f32[4,32,2,6144]{3,0,2,1:T(4,128)} %bitcast.98, pred[32,2]{0,1:T(4,128)(4,1)S(1)} %copy.9), kind=kLoop, calls=%fused_computation.5 | loop fusion | flops 1572864 | bytes 12582976 | tf_op jit(solution)/shard_map/jit(_take)/select_n | solution.py:60
  202.2 2.1 fusion.24
  204.3 3.3 %fusion.7 = f32[32,6144]{1,0:T(8,128)} fusion(f32[4,32,2,6144]{3,0,1,2:T(4,128)S(1)} %copy_select_fusion), kind=kLoop, calls=%fused_computation.26 | loop fusion | flops 196608 | bytes 1572864 | tf_op jit(solution)/shard_map/sub | solution.py:11
  207.6 2.5 %sub.154 = f32[16,2,6144]{2,1,0:T(2,128)} reshape(f32[32,6144]{1,0:T(8,128)} %fusion.7) | data formatting | bytes 1572864 | tf_op jit(solution)/shard_map/sub | solution.py:11
  210.1 3.3 %multiply_add_fusion.1 = f32[4,16,2,6144]{3,0,2,1:T(4,128)S(1)} fusion(f32[4,16,2,6144]{3,0,2,1:T(4,128)} %bitcast.102, f32[4,16,2,6144]{3,0,2,1:T(4,128)S(1)} %bitcast.101, f32[16,2,6144]{2,1,0:T(2,128)} %sub.154), kind=kLoop, calls=%fused_computation.7 | loop fusion | flops 1572864 | bytes 10223616 | tf_op jit(solution)/shard_map/add | solution.py:11
  213.6 1.9 fusion.9
  215.6 1.2 sub.157
  216.8 0.9 fusion.6
  217.8 0.6 fusion.13
  219.7 0.7 pad_maximum_fusion
  220.4 4.0 %all-to-all-start.1 = ((f32[2,4,1,6144]{3,1,2,0:T(4,128)}), f32[2,4,1,6144]{3,1,2,0:T(4,128)S(1)}, u32[]{:S(2)}, u32[]{:S(2)}) async-start(f32[2,4,1,6144]{3,1,2,0:T(4,128)} %pad_maximum_fusion), calls=%async_computation.1 | async-start | bytes 393216 | tf_op jit(solution)/shard_map/all_to_all | solution.py:65
  224.4 0.6 fusion.28
  227.4 3.3 %all-to-all-done.1 = f32[2,4,1,6144]{3,1,2,0:T(4,128)S(1)} async-done(((f32[2,4,1,6144]{3,1,2,0:T(4,128)}), f32[2,4,1,6144]{3,1,2,0:T(4,128)S(1)}, u32[]{:S(2)}, u32[]{:S(2)}) %all-to-all-start.1) | async-done | bytes 196640 | tf_op jit(solution)/shard_map/all_to_all | solution.py:65
  230.8 0.7 fusion.15
  (28 shorter events, 2.5 us)
Async XLA Ops:
  96.8 9.8 %copy-start = (s32[384]{0:T(512)S(1)}, s32[384]{0:T(512)}, u32[]{:S(2)}) copy-start(s32[384]{0:T(512)} %param.5) | copy-start | bytes 4612
  96.8 91.6 %all-to-all-start = ((f32[4,64,6144]{2,0,1:T(4,128)}), f32[4,64,6144]{2,0,1:T(4,128)}, u32[]{:S(2)}, u32[]{:S(2)}) async-start(f32[4,64,6144]{2,0,1:T(4,128)} %multiply_add_fusion), calls=%async_computation | async-start | bytes 12582912 | tf_op jit(solution)/shard_map/all_to_all | solution.py:54
  220.4 10.3 %all-to-all-start.1 = ((f32[2,4,1,6144]{3,1,2,0:T(4,128)}), f32[2,4,1,6144]{3,1,2,0:T(4,128)S(1)}, u32[]{:S(2)}, u32[]{:S(2)}) async-start(f32[2,4,1,6144]{3,1,2,0:T(4,128)} %pad_maximum_fusion), calls=%async_computation.1 | async-start | bytes 393216 | tf_op jit(solution)/shard_map/all_to_all | solution.py:65
